TPU v7x, 32 devices: a whole 2x2x4 slice. The times are simulated.
32 devices in a mesh: gz: 32 (over z, y, x, core).
Axes of the slice: x: 2, y: 2, z: 4, core: 2. Of those that a mesh axis runs over, the one named last changes fastest.
Arguments:
- scores: int32 [128, 512, 512], P('gz'), may hold values from 0 to 33554431, as said below
Outputs:
- status: int32 [128, 512, 512], P('gz')
- counts: int32 [3], replicated
Inputs may be any that keep to these rules, and one draw needn't show every extreme that they name: `scores`: all values distinct: a permutation of 0 to 33554431.
All inputs are finite; a program needn't handle non-finite values.
Results may differ from a plain program's by a relative error of at most 0.000001.
Values may be sent and summed in bfloat16 or wider, within the bound.
A program may use at most 64 MiB of HBM per device.

v0:
```python
import functools

import jax
import jax.numpy as jnp
from jax import lax
from jax.experimental import pallas as pl
from jax.experimental.pallas import tpu as pltpu
from jax.sharding import PartitionSpec as P


AXIS = "gz"
FINE = 16
ROWS = 32
PARTS = 4
PAD = 8
LANES = 128
NONE = -(2.0**126)


def roll(x, shift, axis):
    return pltpu.roll(x, shift % x.shape[axis], axis)


def encode(score, total):
    if total <= 1 << 25:
        return (score - (1 << 24)).astype(jnp.float32)
    value = ((score & ((1 << 23) - 1)) + (1 << 23)).astype(jnp.float32)
    for bit in range(23, (total - 1).bit_length()):
        factor = jnp.where((score & (1 << bit)) != 0, 2.0 ** (1 << (bit - 23)), 1.0)
        value = value * factor
    return value


def spread(load, chunks, op, blank, lane):
    x = [
        op(
            op(op(load(c, -2), load(c, -1)), op(load(c, 0), load(c, 1))),
            load(c, 2),
        )
        for c in range(chunks)
    ]
    one = [roll(v, -1, 1) for v in x] + [blank]
    two = [roll(v, -2, 1) for v in x] + [blank]
    pair = [
        op(x[c], jnp.where(lane >= LANES - 1, one[c + 1], one[c])) for c in range(chunks)
    ]
    before = [jnp.where(lane == 1, roll(x[0], 1, 1), blank)]
    before += [roll(v, 2, 1) for v in pair]
    return [
        op(
            op(pair[c], jnp.where(lane < 2, before[c], before[c + 1])),
            jnp.where(lane >= LANES - 2, two[c + 1], two[c]),
        )
        for c in range(chunks)
    ]


def parity():
    row = lax.broadcasted_iota(jnp.int32, (8, LANES), 0) % 2 == 0
    lane = lax.broadcasted_iota(jnp.int32, (8, LANES), 1) % 2 == 0
    return row, lane


def pack(x):
    row, lane = parity()
    half = len(x) // 2

    def fold(part):
        part = jnp.maximum(part, roll(part, -1, 0))
        return jnp.maximum(part, roll(part, -1, 1))

    out = []
    for c in range(half):
        rows = []
        for r in range(0, x[0].shape[0], 16):
            quads = [
                jnp.where(
                    lane, fold(x[c][k : k + 8]), roll(fold(x[c + half][k : k + 8]), 1, 1)
                )
                for k in (r, r + 8)
            ]
            rows.append(jnp.where(row, quads[0], roll(quads[1], 1, 0)))
        out.append(jnp.concatenate(rows, axis=0))
    return out


def unpack(x):
    row, lane = parity()
    low, high = [], []
    for v in x:
        lows, highs = [], []
        for r in range(0, v.shape[0], 8):
            part = v[r : r + 8]
            for rows in (
                jnp.where(row, part, roll(part, 1, 0)),
                jnp.where(row, roll(part, -1, 0), part),
            ):
                lows.append(jnp.where(lane, rows, roll(rows, 1, 1)))
                highs.append(jnp.where(lane, roll(rows, -1, 1), rows))
        low.append(jnp.concatenate(lows, axis=0))
        high.append(jnp.concatenate(highs, axis=0))
    return low + high


def kernel(
    n, scores, packed_status, counts, field, near, bits, found, cand_send, cand_recv,
    resp_send, resp_recv, tally, cnt_send, cnt_recv, send_sem, recv_sem,
    cnt_send_sem, cnt_recv_sem,
):
    depth, nx, ny = scores.shape
    total = n * depth * nx * ny
    chunks = ny // LANES
    me = lax.axis_index(AXIS)
    has = (me > 0, me < n - 1)
    lone = tuple(jnp.where(h, 0, 1).astype(jnp.int32) for h in has)
    edge = ((0, 1), (depth - 2, depth - 1))
    halo_bits = ((0, 1), (depth + 2, depth + 3))
    lane = lax.broadcasted_iota(jnp.int32, (FINE, LANES), 1)

    def spot(rows):
        shape = (rows, LANES)
        row = lax.broadcasted_iota(jnp.int32, shape, 0) % 2
        return row * 2 + lax.broadcasted_iota(jnp.int32, shape, 1) % 2

    part_rows = nx // PARTS
    columns = [slice(c * LANES, (c + 1) * LANES) for c in range(chunks)]

    barrier = pltpu.get_barrier_semaphore()

    @pl.loop(1, n)
    def _(i):
        pl.semaphore_signal(
            barrier,
            inc=1,
            device_id=(lax.rem(me + i, n),),
            device_id_type=pl.DeviceIdType.MESH,
        )

    for rows in (slice(0, PAD), slice(PAD + nx, 2 * PAD + nx)):
        field[:, :, rows, :] = jnp.full((depth, chunks, PAD, LANES), NONE, jnp.float32)
        bits[:, rows, :] = jnp.zeros((chunks, PAD, LANES), jnp.int32)
    tally[...] = jnp.zeros_like(tally)
    for side in range(2):

        @pl.when(jnp.logical_not(has[side]))
        def _():
            for phase in range(2):
                cand_recv[phase, side] = jnp.full(cand_recv.shape[2:], -1, jnp.int32)
                resp_recv[phase, side] = jnp.ones(resp_recv.shape[2:], jnp.bfloat16)

    @pl.loop(0, nx // ROWS)
    def _(block):
        top = pl.multiple_of(block * ROWS, ROWS)
        for z in range(depth):
            for c in range(chunks):
                field[z, c, pl.ds(pl.multiple_of(top + PAD, PAD), ROWS), :] = encode(
                    scores[z, pl.ds(top, ROWS), columns[c]], total
                )

    pl.semaphore_wait(barrier, n - 1)

    def exchange(send, recv, phase, step, side, part, arrival):
        rows = pl.ds(pl.multiple_of(part * (part_rows // 2), part_rows // 2), part_rows // 2)
        there = arrival if arrival is not None else 1 - side
        return pltpu.make_async_remote_copy(
            src_ref=send.at[phase, side, rows, :],
            dst_ref=recv.at[phase, there, rows, :],
            send_sem=send_sem.at[step, side, part],
            recv_sem=recv_sem.at[step, there, part],
            device_id=(me + (1 if side else -1),),
            device_id_type=pl.DeviceIdType.MESH,
        )

    def start(send, recv, phase, step, part):
        for side in range(2):

            @pl.when(has[side])
            def _():
                exchange(send, recv, phase, step, side, part, None).start()

    def finish(send, recv, phase, step, part):
        for side in range(2):

            @pl.when(has[side])
            def _():
                exchange(send, recv, phase, step, side, part, None).wait_send()
                exchange(send, recv, phase, step, side, part, side).wait_recv()

    def search(phase, part):
        place = spot(FINE)

        @pl.loop(0, part_rows // FINE)
        def _(block):
            top = pl.multiple_of(part * part_rows + block * FINE, FINE)
            here = pl.ds(top, FINE)
            wide = [
                spread(
                    lambda c, d: field[z, c, pl.ds(top + (PAD + d), FINE), :],
                    chunks, jnp.maximum, NONE, lane,
                )
                for z in range(depth)
            ]
            codes = ([], [])
            count = jnp.zeros((FINE, LANES), jnp.int32)
            for c in range(chunks):
                w = [wide[z][c] for z in range(depth)]
                low, high = jnp.maximum(w[0], w[1]), jnp.maximum(w[-1], w[-2])
                near[0, 0, c, here, :] = w[0]
                near[0, 1, c, here, :] = low
                near[1, 0, c, here, :] = high
                near[1, 1, c, here, :] = w[-1]
                own = jnp.zeros((FINE, LANES), jnp.int32)
                best = []
                for z in range(depth):
                    value = field[z, c, pl.ds(pl.multiple_of(top + PAD, PAD), FINE), :]
                    terms = {k: w[k] for k in range(max(z - 2, 0), min(z + 3, depth))}
                    if 0 in terms and 1 in terms:
                        terms[0] = low
                        del terms[1]
                    if depth - 1 in terms and depth - 2 in terms:
                        terms[depth - 1] = high
                        del terms[depth - 2]
                    is_best = value == functools.reduce(jnp.maximum, list(terms.values()))
                    if phase:
                        is_best = is_best & (value > NONE)
                    own = own | jnp.where(is_best, 4 << z, 0)
                    best.append(is_best)
                found[c, here, :] = own
                for side in range(2):
                    a, b = edge[side]
                    held_a = scores[a, here, columns[c]]
                    held_b = scores[b, here, columns[c]]
                    codes[side].append(
                        jnp.where(
                            best[a],
                            held_a * 8 + place,
                            jnp.where(best[b], held_b * 8 + (place + 4), -1),
                        )
                    )
                if phase:
                    for side in range(2):
                        for z in edge[side]:
                            count = count + jnp.where(best[z], lone[side], 0)
                    for z in range(2, depth - 2):
                        count = count + jnp.where(best[z], 1, 0)
            small = pl.ds(pl.multiple_of(top // 2, FINE // 2), FINE // 2)
            for side in range(2):
                for c, v in enumerate(pack(codes[side])):
                    cand_send[phase, side, small, columns[c]] = v
            if phase:
                tally[2, :FINE] += count

    def judge(phase, part):
        place = spot(ROWS)

        @pl.loop(0, part_rows // ROWS)
        def _(block):
            top = pl.multiple_of(part * part_rows + block * ROWS, ROWS)
            small = pl.ds(pl.multiple_of(top // 2, ROWS // 2), ROWS // 2)
            here = pl.ds(top, ROWS)
            halo = [jnp.zeros((ROWS, LANES), jnp.int32) for _ in range(chunks)]
            count = jnp.zeros((ROWS, LANES), jnp.int32)
            for side in range(2):
                codes = unpack(
                    [cand_recv[phase, side, small, columns[c]] for c in range(chunks // 2)]
                )
                verdicts = []
                for c, code in enumerate(codes):
                    where = code & 7
                    score = jnp.where(code < 0, NONE, encode(code >> 3, total))
                    low = (where == place) & (score > near[side, 0, c, here, :])
                    high = (where == place + 4) & (score > near[side, 1, c, here, :])
                    alive = jnp.where(low | high, 1, 0)
                    verdicts.append(alive)
                    if phase:
                        count = count + alive
                    else:
                        halo[c] = halo[c] | jnp.where(low, 1 << halo_bits[side][0], 0)
                        halo[c] = halo[c] | jnp.where(high, 1 << halo_bits[side][1], 0)
                for c, v in enumerate(pack(verdicts)):
                    resp_send[phase, side, small, columns[c]] = v.astype(
                        jnp.float32
                    ).astype(jnp.bfloat16)
            if phase:
                tally[2] += count
            else:
                for c in range(chunks):
                    bits[c, pl.ds(pl.multiple_of(top + PAD, PAD), ROWS), :] = halo[c]

    def confirmed(phase, top):
        small = pl.ds(pl.multiple_of(top // 2, ROWS // 2), ROWS // 2)
        own = [found[c, pl.ds(top, ROWS), :] for c in range(chunks)]
        for side in range(2):
            verdicts = unpack(
                [
                    resp_recv[phase, side, small, columns[c]].astype(jnp.float32)
                    for c in range(chunks // 2)
                ]
            )
            mask = (4 << edge[side][0]) | (4 << edge[side][1])
            own = [jnp.where(v > 0.5, o, o & ~mask) for v, o in zip(verdicts, own)]
        return own

    def settle(part):
        @pl.loop(0, part_rows // ROWS)
        def _(block):
            top = pl.multiple_of(part * part_rows + block * ROWS, ROWS)
            for c, own in enumerate(confirmed(0, top)):
                bits[c, pl.ds(pl.multiple_of(top + PAD, PAD), ROWS), :] |= own

    def remove(part):
        @pl.loop(0, part_rows // FINE)
        def _(block):
            top = pl.multiple_of(part * part_rows + block * FINE, FINE)
            centre = pl.ds(pl.multiple_of(top + PAD, PAD), FINE)
            reach = spread(
                lambda c, d: bits[c, pl.ds(top + (PAD + d), FINE), :],
                chunks, jnp.bitwise_or, 0, lane,
            )
            first, second = tally[0, :FINE], tally[1, :FINE]
            for c in range(chunks):
                roots = bits[c, centre, :]
                status = jnp.zeros((FINE, LANES), jnp.int32)
                for z in range(depth):
                    is_root = (roots & (4 << z)) != 0
                    covered = (reach[c] & (31 << z)) != 0
                    field[z, c, centre, :] = jnp.where(covered, NONE, field[z, c, centre, :])
                    status = status | jnp.where(
                        is_root, 1 << (2 * z), jnp.where(covered, 2 << (2 * z), 0)
                    )
                    first = first + jnp.where(is_root, 1, 0)
                    second = second + jnp.where(covered, 1, 0)
                packed_status[pl.ds(top, FINE), columns[c]] = status
            tally[0, :FINE] = first
            tally[1, :FINE] = second

    for phase in range(2):

        @pl.loop(0, PARTS)
        def _(part):
            search(phase, part)
            start(cand_send, cand_recv, phase, 2 * phase, part)

        @pl.loop(0, PARTS)
        def _(part):
            finish(cand_send, cand_recv, phase, 2 * phase, part)
            judge(phase, part)
            start(resp_send, resp_recv, phase, 2 * phase + 1, part)

        if phase == 0:

            @pl.loop(0, PARTS)
            def _(part):
                finish(resp_send, resp_recv, 0, 1, part)
                settle(part)

                @pl.when(part > 0)
                def _():
                    remove(part - 1)

            remove(PARTS - 1)

    roots, covered, late = (jnp.sum(tally[i]) for i in range(3))
    cells = depth * nx * ny
    column = lax.broadcasted_iota(jnp.int32, cnt_send.shape, 1)
    mine = jnp.where(
        column == 0,
        cells - roots,
        jnp.where(column == 1, cells - covered, cells - covered - late),
    )
    cnt_send[...] = mine

    def report(i):
        return pltpu.make_async_remote_copy(
            src_ref=cnt_send,
            dst_ref=cnt_recv.at[i],
            send_sem=cnt_send_sem.at[i],
            recv_sem=cnt_recv_sem.at[i],
            device_id=(lax.rem(me + i, n),),
            device_id_type=pl.DeviceIdType.MESH,
        )

    @pl.loop(1, n)
    def _(i):
        report(i).start()

    @pl.loop(0, PARTS)
    def _(part):
        finish(resp_send, resp_recv, 1, 3, part)

        @pl.loop(0, part_rows // ROWS)
        def _(block):
            top = pl.multiple_of(part * part_rows + block * ROWS, ROWS)
            for c, own in enumerate(confirmed(1, top)):
                status = packed_status[pl.ds(top, ROWS), columns[c]]
                for z in range(depth):
                    status = status | jnp.where((own & (4 << z)) != 0, 1 << (2 * z), 0)
                packed_status[pl.ds(top, ROWS), columns[c]] = status

    @pl.loop(1, n)
    def _(i):
        report(i).wait()

    cnt_recv[0] = mine
    counts[...] = jnp.sum(cnt_recv[...], axis=0)


def shards(scores):
    depth, nx, ny = scores.shape
    n = lax.axis_size(AXIS)
    vmem = pltpu.VMEM
    small = (nx // 2, ny // 2)
    chunks = ny // LANES
    packed_status, counts = pl.pallas_call(
        functools.partial(kernel, n),
        out_shape=(
            jax.ShapeDtypeStruct((nx, ny), jnp.int32),
            jax.ShapeDtypeStruct((8, 128), jnp.int32),
        ),
        in_specs=[pl.BlockSpec(memory_space=vmem)],
        out_specs=(pl.BlockSpec(memory_space=vmem),) * 2,
        scratch_shapes=[
            vmem((depth, chunks, nx + 2 * PAD, LANES), jnp.float32),
            vmem((2, 2, chunks, nx, LANES), jnp.float32),
            vmem((chunks, nx + 2 * PAD, LANES), jnp.int32),
            vmem((chunks, nx, LANES), jnp.int32),
            vmem((2, 2) + small, jnp.int32),
            vmem((2, 2) + small, jnp.int32),
            vmem((2, 2) + small, jnp.bfloat16),
            vmem((2, 2) + small, jnp.bfloat16),
            vmem((3, ROWS, LANES), jnp.int32),
            vmem((8, 128), jnp.int32),
            vmem((n, 8, 128), jnp.int32),
            pltpu.SemaphoreType.DMA((4, 2, PARTS)),
            pltpu.SemaphoreType.DMA((4, 2, PARTS)),
            pltpu.SemaphoreType.DMA((n,)),
            pltpu.SemaphoreType.DMA((n,)),
        ],
        compiler_params=pltpu.CompilerParams(
            collective_id=0, has_side_effects=True, vmem_limit_bytes=48 * 1024 * 1024
        ),
    )(scores)
    place = 2 * jnp.arange(depth, dtype=jnp.int32)[:, None, None]
    return (packed_status[None] >> place) & 3, counts[0, :3]


def solution(mesh):
    return jax.shard_map(
        shards,
        mesh=mesh,
        in_specs=(P(AXIS, None, None),),
        out_specs=(P(AXIS, None, None), P()),
        check_vma=False,
    )
```

profile of v0, /device:TPU:0, one launch (start us, length us, event | category | flops | bytes accessed | tf_op | source)
XLA Modules:
  0.0 56.9 jit_solution(12838139570315745319)
XLA Ops:
  0.6 0.0 copy-start
  0.7 2.2 %copy-done = s32[4,512,512]{2,1,0:T(8,128)S(1)} copy-done((s32[4,512,512]{2,1,0:T(8,128)S(1)}, s32[4,512,512]{2,1,0:T(8,128)}, u32[]{:S(2)}) %copy-start) | copy-done | bytes 4194328
  2.8 50.9 %shard_map.30 = (s32[512,512]{1,0:T(8,128)S(1)}, s32[8,128]{1,0:T(8,128)S(1)}) custom-call(s32[4,512,512]{2,1,0:T(8,128)S(1)} %copy-done), custom_call_target="tpu_custom_call" | custom-call | tf_op jit(solution)/shard_map/pallas_call | solution.py:414
  53.7 0.5 slice_bitcast_fusion
  54.2 2.6 %shift-right-arithmetic_and_fusion = s32[4,512,512]{2,1,0:T(8,128)} fusion(s32[4]{0:T(128)S(1)} %iota_multiply_fusion, s32[512,512]{1,0:T(8,128)S(1)} %get-tuple-element.4), kind=kLoop, calls=%fused_computation | loop fusion | flops 2097152 | bytes 5242896 | tf_op jit(solution)/shard_map/and | solution.py:444
  (1 shorter events, 0.0 us)
Async XLA Ops:
  0.6 2.2 %copy-start = (s32[4,512,512]{2,1,0:T(8,128)S(1)}, s32[4,512,512]{2,1,0:T(8,128)}, u32[]{:S(2)}) copy-start(s32[4,512,512]{2,1,0:T(8,128)} %scores.1) | copy-start | bytes 12582916
where the time goes:
time: 57 us; the launch traced here: 56.9 us
  Pallas kernels  50.9 us (89%)
  local copies, waits for them, and re-layouts  2.7 us (5%)
  other arithmetic  2.64 us (5%)
  between operations  0.65 us (1%)
    pallas_call x1, Pallas kernels, shards(): pl.pallas_call(functools.partial(kernel, n), out_shape=(jax.ShapeDtypeStr...  50.9 us
    and x1, other arithmetic, shards(): return (packed_status[None] >> place & 3, counts[0, :3])  2.64 us
    unnamed x2, local copies, waits for them, and re-layouts  2.18 us

commit v1 on v0

--- a/solution.py
+++ b/solution.py
@@ -9,8 +9,8 @@
 
 
 AXIS = "gz"
-FINE = 16
-ROWS = 32
+FINE = 32
+ROWS = 64
 PARTS = 4
 PAD = 8
 LANES = 128
@@ -334,31 +334,41 @@
             tally[0, :FINE] = first
             tally[1, :FINE] = second
 
-    for phase in range(2):
-
-        @pl.loop(0, PARTS)
-        def _(part):
-            search(phase, part)
-            start(cand_send, cand_recv, phase, 2 * phase, part)
-
-        @pl.loop(0, PARTS)
-        def _(part):
-            finish(cand_send, cand_recv, phase, 2 * phase, part)
-            judge(phase, part)
-            start(resp_send, resp_recv, phase, 2 * phase + 1, part)
-
-        if phase == 0:
-
-            @pl.loop(0, PARTS)
-            def _(part):
-                finish(resp_send, resp_recv, 0, 1, part)
-                settle(part)
-
-                @pl.when(part > 0)
-                def _():
-                    remove(part - 1)
-
-            remove(PARTS - 1)
+    def offer(phase, part):
+        search(phase, part)
+        start(cand_send, cand_recv, phase, 2 * phase, part)
+
+    def answer(phase, part):
+        finish(cand_send, cand_recv, phase, 2 * phase, part)
+        judge(phase, part)
+        start(resp_send, resp_recv, phase, 2 * phase + 1, part)
+
+    @pl.loop(0, PARTS)
+    def _(part):
+        offer(0, part)
+
+    @pl.loop(0, PARTS)
+    def _(part):
+        answer(0, part)
+
+    @pl.loop(0, PARTS + 2)
+    def _(part):
+        @pl.when(part < PARTS)
+        def _():
+            finish(resp_send, resp_recv, 0, 1, part)
+            settle(part)
+
+        @pl.when((part > 0) & (part <= PARTS))
+        def _():
+            remove(part - 1)
+
+        @pl.when(part > 1)
+        def _():
+            offer(1, part - 2)
+
+    @pl.loop(0, PARTS)
+    def _(part):
+        answer(1, part)
 
     roots, covered, late = (jnp.sum(tally[i]) for i in range(3))
     cells = depth * nx * ny

time: 57 us -> 47.6 us (0.84)
  Pallas kernels: 50.9 us -> 41.5 us
    pallas_call x1, Pallas kernels: 50.9 us -> 41.5 us  [shards(): pl.pallas_call(functools.partial(kernel, n), out_shape=(jax.ShapeDtypeStr...]
where the time goes in v1:
time: 47.6 us; the launch traced here: 47.5 us
  Pallas kernels  41.5 us (87%)
  local copies, waits for them, and re-layouts  2.7 us (6%)
  other arithmetic  2.64 us (6%)
  between operations  0.65 us (1%)
    pallas_call x1, Pallas kernels, shards(): pl.pallas_call(functools.partial(kernel, n), out_shape=(jax.ShapeDtypeStr...  41.5 us
    and x1, other arithmetic, shards(): return (packed_status[None] >> place & 3, counts[0, :3])  2.64 us
    unnamed x2, local copies, waits for them, and re-layouts  2.18 us

profile of v1, /device:TPU:0, one launch (start us, length us, event | category | flops | bytes accessed | tf_op | source)
XLA Modules:
  0.0 47.5 jit_solution(12616664265776750815)
XLA Ops:
  0.6 0.0 copy-start
  0.7 2.2 %copy-done = s32[4,512,512]{2,1,0:T(8,128)S(1)} copy-done((s32[4,512,512]{2,1,0:T(8,128)S(1)}, s32[4,512,512]{2,1,0:T(8,128)}, u32[]{:S(2)}) %copy-start) | copy-done | bytes 4194328
  2.8 41.5 %shard_map.30 = (s32[512,512]{1,0:T(8,128)S(1)}, s32[8,128]{1,0:T(8,128)S(1)}) custom-call(s32[4,512,512]{2,1,0:T(8,128)S(1)} %copy-done), custom_call_target="tpu_custom_call" | custom-call | tf_op jit(solution)/shard_map/pallas_call | solution.py:424
  44.3 0.5 %slice_bitcast_fusion = s32[3]{0:T(128)} fusion(s32[8,128]{1,0:T(8,128)S(1)} %get-tuple-element.5), kind=kLoop, calls=%fused_computation.1 | loop fusion | bytes 24 | tf_op jit(solution)/shard_map/squeeze | solution.py:454
  44.8 2.6 %shift-right-arithmetic_and_fusion = s32[4,512,512]{2,1,0:T(8,128)} fusion(s32[4]{0:T(128)S(1)} %iota_multiply_fusion, s32[512,512]{1,0:T(8,128)S(1)} %get-tuple-element.4), kind=kLoop, calls=%fused_computation | loop fusion | flops 2097152 | bytes 5242896 | tf_op jit(solution)/shard_map/and | solution.py:454
  (1 shorter events, 0.0 us)
Async XLA Ops:
  0.6 2.2 %copy-start = (s32[4,512,512]{2,1,0:T(8,128)S(1)}, s32[4,512,512]{2,1,0:T(8,128)}, u32[]{:S(2)}) copy-start(s32[4,512,512]{2,1,0:T(8,128)} %scores.1) | copy-start | bytes 12582916
